TPU v7x, 16 devices: a 4x2x1 block of a 4x4x8 slice. The times are simulated.
16 devices in a mesh: rep: 4 (over y, z, core), pp: 4 (over x).
Axes of the slice: x: 4, y: 2, z: 1, core: 2. Of those that a mesh axis runs over, the one named last changes fastest.
The devices are a block of a 4x4x8 slice.
Arguments:
- x: bfloat16 [32, 512, 512], P('rep'), parts along dimension 0
- dy: bfloat16 [32, 512, 512], P('rep'), parts along dimension 0
- w_gate: bfloat16 [4, 512, 1280], P('pp')
- w_up: bfloat16 [4, 512, 1280], P('pp')
- w_down: bfloat16 [4, 1280, 512], P('pp')
Outputs:
- output 1: bfloat16 [16, 512, 1280], P(('rep', 'pp')), parts along dimension 0
- output 2: bfloat16 [16, 512, 1280], P(('rep', 'pp')), parts along dimension 0
- output 3: bfloat16 [16, 1280, 512], P(('rep', 'pp')), parts along dimension 0
There are 4 independent parts. A program takes and returns all parts, laid end to end along the dimension named above; an argument that names none is the same for every part.
All inputs are finite; a program needn't handle non-finite values.
Results may differ from a plain program's by a relative error of at most 0.018.
Values are sent between devices in bfloat16 or wider.
A program may use at most 768 MiB of HBM per device.

v0:
```python
import functools

import jax
import jax.numpy as jnp
from jax import lax
from jax.experimental import pallas as pl
from jax.experimental.pallas import tpu as pltpu
from jax.sharding import PartitionSpec as P

MESH = pl.DeviceIdType.MESH
ROWS = 128
COLS = 256
LAG = 5
SENDS = 3
f32, bf16 = jnp.float32, jnp.bfloat16


def dot(a, b):
    return jnp.dot(a, b, preferred_element_type=f32)


def sigmoid(r):
    return 0.5 * jnp.tanh(0.5 * r) + 0.5


def kernel(stages, micro, tokens, x, dy, wg, wu, wd, out_g, out_u, out_d,
           fwd_in, bwd_in, fwd_out, bwd_out, g_ring, u_ring, act, dg, du, actc, a_t, dy_t,
           wg_v, wu_v, wd_v, wg_t, wu_t, wd_t, acc,
           fwd_sem, bwd_sem, fwd_send, bwd_send, w_sem, o_sem):
    me = lax.axis_index("pp")
    per = tokens // ROWS
    chunks = micro * per
    d, ff = wg_v.shape
    ring = g_ring.shape[0]
    first, last = me == 0, me == stages - 1
    lag = LAG * (stages - 1 - me)

    def load_x(i):
        return pltpu.make_async_copy(x.at[i // per, pl.ds(lax.rem(i, per) * ROWS, ROWS), :], fwd_in.at[i], fwd_sem.at[i])

    def load_dy(i):
        return pltpu.make_async_copy(dy.at[i // per, pl.ds(lax.rem(i, per) * ROWS, ROWS), :], bwd_in.at[i], bwd_sem.at[i])

    def onward(i):
        slot = lax.rem(i, SENDS)
        return pltpu.make_async_remote_copy(
            src_ref=fwd_out.at[slot], dst_ref=fwd_in.at[i], send_sem=fwd_send.at[slot], recv_sem=fwd_sem.at[i],
            device_id={"pp": me + 1}, device_id_type=MESH)

    def back(i):
        slot = lax.rem(i, SENDS)
        return pltpu.make_async_remote_copy(
            src_ref=bwd_out.at[slot], dst_ref=bwd_in.at[i], send_sem=bwd_send.at[slot], recv_sem=bwd_sem.at[i],
            device_id={"pp": me - 1}, device_id_type=MESH)

    loads = [pltpu.make_async_copy(src.at[0], dst, w_sem.at[n]) for n, (src, dst) in enumerate(((wg, wg_v), (wu, wu_v), (wd, wd_v)))]

    @pl.when(first)
    def _():
        load_x(0).start()
    for load in loads:
        load.start()

    @pl.when(first)
    def _():
        def go(i, c):
            load_x(i).start()
            return c
        lax.fori_loop(1, chunks, go, 0)

    @pl.when(last)
    def _():
        def go(i, c):
            load_dy(i).start()
            return c
        lax.fori_loop(0, chunks, go, 0)

    barrier = pltpu.get_barrier_semaphore()

    @pl.when(~first)
    def _():
        pl.semaphore_signal(barrier, inc=1, device_id={"pp": me - 1}, device_id_type=MESH)

    @pl.when(~last)
    def _():
        pl.semaphore_signal(barrier, inc=1, device_id={"pp": me + 1}, device_id_type=MESH)

    pl.semaphore_wait(barrier, jnp.where(first | last, 1, 2))

    for load in loads:
        load.wait()

    def turn(src, dst):
        def go(b, c):
            rows = pl.ds(pl.multiple_of(b * ROWS, ROWS), ROWS)
            dst[:, rows] = src[rows, :].T
            return c
        lax.fori_loop(0, src.shape[0] // ROWS, go, 0)

    @pl.when(~first)
    def _():
        turn(wd_v, wd_t)
        turn(wg_v, wg_t)
        turn(wu_v, wu_t)

    def norm(h):
        wide = h.astype(f32)
        scale = lax.rsqrt(jnp.sum(wide * wide, -1, keepdims=True) * (1.0 / d) + 1e-6)
        return wide, scale

    def forward(i):
        @pl.when(first)
        def _():
            load_x(i).wait()

        @pl.when(~first)
        def _():
            onward(i).wait_recv()
        slot = lax.rem(i, ring)
        h = fwd_in[i]
        wide, scale = norm(h)
        a = (wide * scale).astype(bf16)
        for t in range(0, ff, COLS):
            cols = slice(t, t + COLS)
            r = dot(a, wg_v[:, cols])
            s = dot(a, wu_v[:, cols])
            g_ring[slot, :, cols] = r
            u_ring[slot, :, cols] = s
            actc[:, cols] = (r * sigmoid(r) * s).astype(bf16)

        @pl.when(~last)
        def _():
            out = lax.rem(i, SENDS)
            y = dot(actc[...], wd_v[...]).astype(bf16)

            @pl.when(i >= SENDS)
            def _():
                onward(i - SENDS).wait_send()
            fwd_out[out] = (fwd_in[i].astype(f32) + y.astype(f32)).astype(bf16)
            onward(i).start()

    def backward(i):
        @pl.when(last)
        def _():
            load_dy(i).wait()

        @pl.when(~last)
        def _():
            back(i).wait_recv()
        slot, m, c = lax.rem(i, ring), lax.rem(i // per, 2), lax.rem(i, per)
        rows = pl.ds(pl.multiple_of(c * ROWS, ROWS), ROWS)
        by_y = bwd_in[i]
        wide, scale = norm(fwd_in[i])
        a_t[m, :, rows] = (wide * scale).astype(bf16).T
        dy_t[m, :, rows] = by_y.T
        for t in range(0, ff, COLS):
            cols = slice(t, t + COLS)
            by = dot(by_y, wd_t[:, cols]).astype(bf16).astype(f32)
            r, s = g_ring[slot, :, cols], u_ring[slot, :, cols]
            v = sigmoid(r)
            t_ = r * v
            act[m, rows, cols] = (t_ * s).astype(bf16)
            du[m, rows, cols] = (t_ * by).astype(bf16)
            bj = by * s
            dg[m, rows, cols] = (bj * v + (r * bj) * (v * (1.0 - v))).astype(bf16)

        @pl.when(~first)
        def _():
            out = lax.rem(i, SENDS)
            by_a = dot(du[m, rows, :], wu_t[...]).astype(bf16).astype(f32)
            by_a = (by_a + dot(dg[m, rows, :], wg_t[...]).astype(bf16).astype(f32)).astype(bf16).astype(f32)
            wide, scale = norm(fwd_in[i])
            along = jnp.sum(wide * by_a, -1, keepdims=True)
            by_h = (by_a * scale + (along * (scale * scale * scale * (-1.0 / d))) * wide).astype(bf16)

            @pl.when(i >= SENDS)
            def _():
                back(i - SENDS).wait_send()
            bwd_out[out] = (bwd_in[i].astype(f32) + by_h.astype(f32)).astype(bf16)
            back(i).start()

    outs = ((out_g, dg), (out_u, du), (out_d, act))

    def put(n, m, rows):
        hbm, stage = outs[n]
        return pltpu.make_async_copy(stage.at[m, rows, :], hbm.at[0, rows, :], o_sem.at[n])

    def weights(i):
        number, q = i // per, lax.rem(i, per)
        m = lax.rem(number, 2)
        rows = pl.ds(pl.multiple_of(q * ROWS, ROWS), ROWS)
        for n, (left, right) in enumerate(((a_t, dg), (a_t, du), (dy_t, act))):
            term = dot(left[m, rows, :], right[m]).astype(bf16).astype(f32)
            acc[n, rows, :] = jnp.where(number == 0, 0.0, acc[n, rows, :]) + term

        @pl.when(number == micro - 1)
        def _():
            for n in range(3):
                outs[n][1][1 - m, rows, :] = acc[n, rows, :].astype(bf16)
                put(n, 1 - m, rows).start()

    def step(i, carry):
        @pl.when(i < chunks)
        def _():
            forward(i)

        @pl.when(first & (i == 2))
        def _():
            turn(wd_v, wd_t)
        j = i - lag

        @pl.when((j >= 0) & (j < chunks))
        def _():
            backward(j)
        k = j - per

        @pl.when((k >= 0) & (k < chunks))
        def _():
            weights(k)
        return carry

    lax.fori_loop(0, chunks + LAG * (stages - 1) + per, step, 0)

    for n in range(SENDS):
        @pl.when(~last)
        def _():
            onward(chunks - SENDS + n).wait_send()

        @pl.when(~first)
        def _():
            back(chunks - SENDS + n).wait_send()
    m = (micro - 1) % 2
    for n in range(3):
        pltpu.make_async_copy(outs[n][1].at[1 - m], outs[n][0].at[0], o_sem.at[n]).wait()


def solution(mesh):
    stages = mesh.shape["pp"]

    def step(x, dy, wg, wu, wd):
        micro, tokens, d = x.shape
        ff = wg.shape[2]
        chunks = micro * (tokens // ROWS)
        ring = LAG * (stages - 1) + 1
        hbm = pl.BlockSpec(memory_space=pl.ANY)
        grad = jax.ShapeDtypeStruct((1, d, ff), bf16)
        g, u, down = pl.pallas_call(
            functools.partial(kernel, stages, micro, tokens),
            out_shape=(grad, grad, grad),
            in_specs=[hbm] * 5,
            out_specs=(hbm,) * 3,
            scratch_shapes=[
                pltpu.VMEM((chunks, ROWS, d), bf16),
                pltpu.VMEM((chunks, ROWS, d), bf16),
                pltpu.VMEM((SENDS, ROWS, d), bf16),
                pltpu.VMEM((SENDS, ROWS, d), bf16),
                pltpu.VMEM((ring, ROWS, ff), f32),
                pltpu.VMEM((ring, ROWS, ff), f32),
                pltpu.VMEM((2, tokens, ff), bf16),
                pltpu.VMEM((2, tokens, ff), bf16),
                pltpu.VMEM((2, tokens, ff), bf16),
                pltpu.VMEM((ROWS, ff), bf16),
                pltpu.VMEM((2, d, tokens), bf16),
                pltpu.VMEM((2, d, tokens), bf16),
                pltpu.VMEM((d, ff), bf16),
                pltpu.VMEM((d, ff), bf16),
                pltpu.VMEM((ff, d), bf16),
                pltpu.VMEM((ff, d), bf16),
                pltpu.VMEM((ff, d), bf16),
                pltpu.VMEM((d, ff), bf16),
                pltpu.VMEM((3, d, ff), f32),
                pltpu.SemaphoreType.DMA((chunks,)),
                pltpu.SemaphoreType.DMA((chunks,)),
                pltpu.SemaphoreType.DMA((SENDS,)),
                pltpu.SemaphoreType.DMA((SENDS,)),
                pltpu.SemaphoreType.DMA((3,)),
                pltpu.SemaphoreType.DMA((3,)),
            ],
            compiler_params=pltpu.CompilerParams(collective_id=0, has_side_effects=True, vmem_limit_bytes=67_043_328),
        )(x, dy, wg, wu, wd)
        return g, u, down.swapaxes(1, 2)

    return jax.shard_map(
        step,
        mesh=mesh,
        in_specs=(P("rep", None, None),) * 2 + (P("pp", None, None),) * 3,
        out_specs=(P(("rep", "pp"), None, None),) * 3,
        check_vma=False,
    )
```

profile of v0, /device:TPU:120, one launch (start us, length us, event | category | flops | bytes accessed | tf_op | source)
XLA Modules:
  0.0 143.7 jit_solution(5191712882466167487)
XLA Ops:
  0.6 137.7 %shard_map.76 = (bf16[1,512,1280]{2,1,0:T(8,128)(2,1)}, bf16[1,512,1280]{2,1,0:T(8,128)(2,1)}, bf16[1,512,1280]{2,1,0:T(8,128)(2,1)}) custom-call(bf16[8,512,512]{2,1,0:T(8,128)(2,1)} %x.1, bf16[8,512,512]{2,1,0:T(8,128)(2,1)} %dy.1, bf16[1,512,1280]{2,1,0:T(8,128)(2,1)} %wg.1, bf16[1,512,1280]{2,1,0:T(8,128)(2,1)} %wu.1, bf16[1,1280,512]{2,1,0:T(8,128)(2,1)} %wd.1), custom_call_target="tpu_custom_call" | custom-call | tf_op jit(solution)/shard_map/pallas_call | solution.py:247
  138.3 0.0 copy-start.1
  138.3 2.5 %copy.8 = bf16[1,1280,512]{2,1,0:T(8,128)(2,1)} copy(bf16[1,1280,512]{1,2,0:T(8,128)(2,1)} %bitcast.1) | data formatting | bytes 2621440
  140.9 0.0 copy-done.1
  140.9 0.0 copy-start
  140.9 1.1 copy.11
  141.9 0.7 copy-done
  142.7 1.1 copy.12
Async XLA Ops:
  138.3 2.5 %copy-start.1 = (bf16[1,512,1280]{2,1,0:T(8,128)(2,1)S(1)}, bf16[1,512,1280]{2,1,0:T(8,128)(2,1)}, u32[]{:S(2)}) copy-start(bf16[1,512,1280]{2,1,0:T(8,128)(2,1)} %get-tuple-element.15) | copy-start | bytes 3932164
  140.9 1.8 %copy-start = (bf16[1,512,1280]{2,1,0:T(8,128)(2,1)S(1)}, bf16[1,512,1280]{2,1,0:T(8,128)(2,1)}, u32[]{:S(2)}) copy-start(bf16[1,512,1280]{2,1,0:T(8,128)(2,1)} %get-tuple-element.16) | copy-start | bytes 3932164
where the time goes:
time: 144 us
  Pallas kernels  138 us (96%)
  local copies, waits for them, and re-layouts  5.38 us (4%)
    pallas_call x1, Pallas kernels, step(): pl.pallas_call(functools.partial(kernel, stages, micro, tokens), out_shap...  138 us
    unnamed x7, local copies, waits for them, and re-layouts  5.38 us

commit v1 on v0

v1 whole, which is shorter than its diff:
```python
import functools

import jax
import jax.numpy as jnp
from jax import lax
from jax.experimental import pallas as pl
from jax.experimental.pallas import tpu as pltpu
from jax.sharding import PartitionSpec as P

MESH = pl.DeviceIdType.MESH
ROWS = 128
COLS = 256
LAGS = (13,8,4,0)
SENDS = 3
f32, bf16 = jnp.float32, jnp.bfloat16


def dot(a, b):
    return jnp.dot(a, b, preferred_element_type=f32)


def chunk(c):
    return pl.ds(pl.multiple_of(c * ROWS, ROWS), ROWS)


def kernel(stages, micro, tokens, x, dy, wg, wu, wd,
           acc, act, a_t, dg, du, dy_t,
           fwd_in, bwd_in, fwd_out, bwd_out, t_ring, q_ring,
           wg_v, wu_v, wd_v, wg_t, wu_t, wd_t,
           fwd_sem, bwd_sem, fwd_send, bwd_send, w_sem):
    me = lax.axis_index("pp")
    per = tokens // ROWS
    chunks = micro * per
    d, ff = wg_v.shape
    ring, held = t_ring.shape[0], act.shape[0]
    first, last = me == 0, me == stages - 1
    lag = sum(jnp.where(me == n, by, 0) for n, by in enumerate(LAGS))

    def load_x(i):
        return pltpu.make_async_copy(x.at[i // per, chunk(lax.rem(i, per)), :], fwd_in.at[i], fwd_sem.at[i])

    def load_dy(i):
        return pltpu.make_async_copy(dy.at[i // per, chunk(lax.rem(i, per)), :], bwd_in.at[i], bwd_sem.at[i])

    def onward(i):
        slot = lax.rem(i, SENDS)
        return pltpu.make_async_remote_copy(
            src_ref=fwd_out.at[slot], dst_ref=fwd_in.at[i], send_sem=fwd_send.at[slot], recv_sem=fwd_sem.at[i],
            device_id={"pp": me + 1}, device_id_type=MESH)

    def back(i):
        slot = lax.rem(i, SENDS)
        return pltpu.make_async_remote_copy(
            src_ref=bwd_out.at[slot], dst_ref=bwd_in.at[i], send_sem=bwd_send.at[slot], recv_sem=bwd_sem.at[i],
            device_id={"pp": me - 1}, device_id_type=MESH)

    loads = [pltpu.make_async_copy(src.at[0], dst, w_sem.at[n]) for n, (src, dst) in enumerate(((wg, wg_v), (wu, wu_v), (wd, wd_v)))]

    @pl.when(first)
    def _():
        load_x(0).start()
    for load in loads:
        load.start()

    @pl.when(first)
    def _():
        def go(i, c):
            load_x(i).start()
            return c
        lax.fori_loop(1, chunks, go, 0)

    @pl.when(last)
    def _():
        def go(i, c):
            load_dy(i).start()
            return c
        lax.fori_loop(0, chunks, go, 0)

    barrier = pltpu.get_barrier_semaphore()

    @pl.when(~first)
    def _():
        pl.semaphore_signal(barrier, inc=1, device_id={"pp": me - 1}, device_id_type=MESH)

    @pl.when(~last)
    def _():
        pl.semaphore_signal(barrier, inc=1, device_id={"pp": me + 1}, device_id_type=MESH)

    pl.semaphore_wait(barrier, jnp.where(first | last, 1, 2))

    for load in loads:
        load.wait()

    def turn(src, dst):
        def go(b, c):
            dst[:, chunk(b)] = src[chunk(b), :].T
            return c
        lax.fori_loop(0, src.shape[0] // ROWS, go, 0)

    @pl.when(~first)
    def _():
        turn(wd_v, wd_t)
        turn(wg_v, wg_t)
        turn(wu_v, wu_t)

    def norm(h):
        wide = h.astype(f32)
        scale = lax.rsqrt(jnp.sum(wide * wide, -1, keepdims=True) * (1.0 / d) + 1e-6)
        return wide, scale

    def forward_wait(i):
        @pl.when(first)
        def _():
            load_x(i).wait()

        @pl.when(~first)
        def _():
            onward(i).wait_recv()

        @pl.when(~last & (i >= SENDS))
        def _():
            onward(i - SENDS).wait_send()

    def gate_up(i):
        slot, m, rows = lax.rem(i, ring), lax.rem(i // per, held), chunk(lax.rem(i, per))
        wide, scale = norm(fwd_in[i])
        a = (wide * scale).astype(bf16)
        a_t[m, :, rows] = a.T
        for t in range(0, ff, COLS):
            cols = slice(t, t + COLS)
            r, s = dot(a, wg_v[:, cols]), dot(a, wu_v[:, cols])
            v = 0.5 * jnp.tanh(0.5 * r) + 0.5
            silu = r * v
            t_ring[slot, :, cols] = silu
            q_ring[slot, :, cols] = s * (v + silu * (1.0 - v))
            act[m, rows, cols] = (silu * s).astype(bf16)

    def down(i):
        m, rows = lax.rem(i // per, held), chunk(lax.rem(i, per))
        y = dot(act[m, rows, :], wd_v[...]).astype(bf16)
        fwd_out[lax.rem(i, SENDS)] = (fwd_in[i].astype(f32) + y.astype(f32)).astype(bf16)

    def forward_send(i):
        @pl.when(~last)
        def _():
            onward(i).start()

    def backward_wait(i):
        @pl.when(last)
        def _():
            load_dy(i).wait()

        @pl.when(~last)
        def _():
            back(i).wait_recv()

        @pl.when(~first & (i >= SENDS))
        def _():
            back(i - SENDS).wait_send()

    def by_gate_up(i):
        slot, m, rows = lax.rem(i, ring), lax.rem(i // per, 2), chunk(lax.rem(i, per))
        by_y = bwd_in[i]
        dy_t[m, :, rows] = by_y.T
        for t in range(0, ff, COLS):
            cols = slice(t, t + COLS)
            by = dot(by_y, wd_t[:, cols]).astype(bf16).astype(f32)
            du[m, rows, cols] = (t_ring[slot, :, cols] * by).astype(bf16)
            dg[m, rows, cols] = (q_ring[slot, :, cols] * by).astype(bf16)

    def by_input(i):
        m, rows = lax.rem(i // per, 2), chunk(lax.rem(i, per))
        by_a = dot(du[m, rows, :], wu_t[...]).astype(bf16).astype(f32)
        by_a = (by_a + dot(dg[m, rows, :], wg_t[...]).astype(bf16).astype(f32)).astype(bf16).astype(f32)
        wide, scale = norm(fwd_in[i])
        along = jnp.sum(wide * by_a, -1, keepdims=True)
        by_h = (by_a * scale + (along * (scale * scale * scale * (-1.0 / d))) * wide).astype(bf16)
        bwd_out[lax.rem(i, SENDS)] = (bwd_in[i].astype(f32) + by_h.astype(f32)).astype(bf16)

    def backward_send(i):
        @pl.when(~first)
        def _():
            back(i).start()

    def weights(i):
        number, rows = i // per, chunk(lax.rem(i, per))
        m, w = lax.rem(number, 2), lax.rem(number, held)
        for n, (left, right) in enumerate(((a_t.at[w], dg.at[m]), (a_t.at[w], du.at[m]), (dy_t.at[m], act.at[w]))):
            term = dot(left[rows, :], right[...]).astype(bf16).astype(f32)
            acc[n, rows, :] = jnp.where(number == 0, 0.0, acc[n, rows, :]) + term

    def step(i, carry):
        j = i - lag
        k = j - per
        forth, backwards, heavy = i < chunks, (j >= 0) & (j < chunks), (k >= 0) & (k < chunks - per)

        @pl.when(forth)
        def _():
            forward_wait(i)
            gate_up(i)

            @pl.when(~last)
            def _():
                down(i)
            forward_send(i)

        @pl.when(first & (i == 2))
        def _():
            turn(wd_v, wd_t)

        @pl.when(backwards)
        def _():
            backward_wait(j)
            by_gate_up(j)

            @pl.when(~first)
            def _():
                by_input(j)
            backward_send(j)

        @pl.when(heavy)
        def _():
            weights(k)
        return carry

    lax.fori_loop(0, chunks + max(LAGS), step, 0)

    for n in range(SENDS):
        @pl.when(~last)
        def _():
            onward(chunks - SENDS + n).wait_send()

        @pl.when(~first)
        def _():
            back(chunks - SENDS + n).wait_send()


def finish(w, m, acc, act, a_t, dg, du, dy_t, out_g, out_u, out_d, stage, turned, sem):
    d = acc.shape[1]
    copies = []
    for n, (left, right, out) in enumerate(((dy_t.at[m], act.at[w], out_d), (a_t.at[w], dg.at[m], out_g), (a_t.at[w], du.at[m], out_u))):
        for q in range(0, d, ROWS):
            rows = slice(q, q + ROWS)
            term = dot(left[rows, :], right[...]).astype(bf16).astype(f32)
            total = (acc[(n + 2) % 3, rows, :] + term).astype(bf16)
            if n == 0:
                turned[:, rows] = total.T
                copy = pltpu.make_async_copy(turned.at[:, rows], out.at[0, :, rows], sem.at[n, q // ROWS])
            else:
                stage[n - 1, rows, :] = total
                copy = pltpu.make_async_copy(stage.at[n - 1, rows, :], out.at[0, rows, :], sem.at[n, q // ROWS])
            copy.start()
            copies.append(copy)
    for copy in copies:
        copy.wait()


def solution(mesh):
    stages = mesh.shape["pp"]

    def step(x, dy, wg, wu, wd):
        micro, tokens, d = x.shape
        ff = wg.shape[2]
        per = tokens // ROWS
        chunks = micro * per
        ring = max(LAGS) + 1
        held = pl.cdiv(ring - 1 + per, per) + 1
        hbm, vmem = pl.BlockSpec(memory_space=pl.ANY), pl.BlockSpec(memory_space=pltpu.VMEM)
        sums = pl.pallas_call(
            functools.partial(kernel, stages, micro, tokens),
            out_shape=(
                pltpu.VMEM((3, d, ff), f32),
                pltpu.VMEM((held, tokens, ff), bf16),
                pltpu.VMEM((held, d, tokens), bf16),
                pltpu.VMEM((2, tokens, ff), bf16),
                pltpu.VMEM((2, tokens, ff), bf16),
                pltpu.VMEM((2, d, tokens), bf16),
            ),
            in_specs=[hbm] * 5,
            out_specs=(vmem,) * 6,
            scratch_shapes=[
                pltpu.VMEM((chunks, ROWS, d), bf16),
                pltpu.VMEM((chunks, ROWS, d), bf16),
                pltpu.VMEM((SENDS, ROWS, d), bf16),
                pltpu.VMEM((SENDS, ROWS, d), bf16),
                pltpu.VMEM((ring, ROWS, ff), f32),
                pltpu.VMEM((ring, ROWS, ff), f32),
                pltpu.VMEM((d, ff), bf16),
                pltpu.VMEM((d, ff), bf16),
                pltpu.VMEM((ff, d), bf16),
                pltpu.VMEM((ff, d), bf16),
                pltpu.VMEM((ff, d), bf16),
                pltpu.VMEM((d, ff), bf16),
                pltpu.SemaphoreType.DMA((chunks,)),
                pltpu.SemaphoreType.DMA((chunks,)),
                pltpu.SemaphoreType.DMA((SENDS,)),
                pltpu.SemaphoreType.DMA((SENDS,)),
                pltpu.SemaphoreType.DMA((3,)),
            ],
            compiler_params=pltpu.CompilerParams(collective_id=0, has_side_effects=True, vmem_limit_bytes=38 * 2**20),
        )(x, dy, wg, wu, wd)
        return pl.pallas_call(
            functools.partial(finish, (micro - 1) % held, (micro - 1) % 2),
            out_shape=(
                jax.ShapeDtypeStruct((1, d, ff), bf16),
                jax.ShapeDtypeStruct((1, d, ff), bf16),
                jax.ShapeDtypeStruct((1, ff, d), bf16),
            ),
            in_specs=[vmem] * 6,
            out_specs=(hbm,) * 3,
            scratch_shapes=[pltpu.VMEM((2, d, ff), bf16), pltpu.VMEM((ff, d), bf16), pltpu.SemaphoreType.DMA((3, d // ROWS))],
            compiler_params=pltpu.CompilerParams(has_side_effects=True, vmem_limit_bytes=8 * 2**20),
        )(*sums)

    return jax.shard_map(
        step,
        mesh=mesh,
        in_specs=(P("rep", None, None),) * 2 + (P("pp", None, None),) * 3,
        out_specs=(P(("rep", "pp"), None, None),) * 3,
        check_vma=False,
    )
```

time: 144 us -> 131 us (0.910)
  Pallas kernels: 138 us -> 130 us
  local copies, waits for them, and re-layouts: 5.38 us -> 0 us
    pallas_call x1, Pallas kernels: 138 us -> 127 us  [step(): pl.pallas_call(functools.partial(kernel, stages, micro, tokens), out_shap...]
    unnamed x7 -> x0, local copies, waits for them, and re-layouts: 5.38 us -> none
    pallas_call x0 -> x1, Pallas kernels: none -> 3.2 us  [step(): pl.pallas_call(functools.partial(finish, (micro - 1) % held, (micro - 1)...]
where the time goes in v1:
time: 131 us; the launch traced here: 130 us
  Pallas kernels  130 us (99%)
    pallas_call x1, Pallas kernels, step(): pl.pallas_call(functools.partial(kernel, stages, micro, tokens), out_shap...  127 us
    pallas_call x1, Pallas kernels, step(): pl.pallas_call(functools.partial(finish, (micro - 1) % held, (micro - 1)...  3.2 us

profile of v1, /device:TPU:120, one launch (start us, length us, event | category | flops | bytes accessed | tf_op | source)
XLA Modules:
  0.0 130.5 jit_solution(3803611902326055007)
XLA Ops:
  0.6 126.7 %shard_map.76 = (f32[3,512,1280]{2,1,0:T(8,128)S(1)}, bf16[6,512,1280]{2,1,0:T(8,128)(2,1)S(1)}, bf16[6,512,512]{2,1,0:T(8,128)(2,1)S(1)}, bf16[2,512,1280]{2,1,...) custom-call(bf16[8,512,512]{2,1,0:T(8,128)(2,1)} %x.1, bf16[8,512,512]{2,1,0:T(8,128)(2,1)} %dy.1, ...), custom_call_target="tpu_custom_call" | custom-call | tf_op jit(solution)/shard_map/pallas_call | solution.py:269
  127.3 3.2 %shard_map.77 = (bf16[1,512,1280]{2,1,0:T(8,128)(2,1)}, bf16[1,512,1280]{2,1,0:T(8,128)(2,1)}, bf16[1,1280,512]{2,1,0:T(8,128)(2,1)}) custom-call(f32[3,512,1280]{2,1,0:T(8,128)S(1)} %get-tuple-element.9.acc, bf16[6,512,1280]{2,1,0:T(8,128)(2,1)S(1)} %get-tuple-element.10.act, bf16[6,512,512]{2,1,0:T(8,128)(2,1)S(1)} %get-tuple-element.11.a_t, ...), custom_call_target="tpu_custom_call" | custom-call | tf_op jit(solution)/shard_map/pallas_call | solution.py:302

commit v2 on v1

--- a/solution.py
+++ b/solution.py
@@ -23,9 +23,15 @@
     return pl.ds(pl.multiple_of(c * ROWS, ROWS), ROWS)
 
 
+def tiles(a_t, dy_t, dg, du, act):
+    for n, left, right in ((2, dy_t, act), (0, a_t, dg), (1, a_t, du)):
+        for t in range(0, right.shape[1], COLS):
+            yield n, slice(t, t + COLS), left, right
+
+
 def kernel(stages, micro, tokens, x, dy, wg, wu, wd,
-           acc, act, a_t, dg, du, dy_t,
-           fwd_in, bwd_in, fwd_out, bwd_out, t_ring, q_ring,
+           acc, act_out, a_out, dg, du, dy_t, t_ring,
+           fwd_in, bwd_in, fwd_out, bwd_out, q_ring, by_act, act, a_t,
            wg_v, wu_v, wd_v, wg_t, wu_t, wd_t,
            fwd_sem, bwd_sem, fwd_send, bwd_send, w_sem):
     me = lax.axis_index("pp")
@@ -117,11 +123,11 @@
         def _():
             onward(i).wait_recv()
 
-        @pl.when(~last & (i >= SENDS))
+        @pl.when(i >= SENDS)
         def _():
             onward(i - SENDS).wait_send()
 
-    def gate_up(i):
+    def gate_up(i, by_ref=None):
         slot, m, rows = lax.rem(i, ring), lax.rem(i // per, held), chunk(lax.rem(i, per))
         wide, scale = norm(fwd_in[i])
         a = (wide * scale).astype(bf16)
@@ -131,32 +137,27 @@
             r, s = dot(a, wg_v[:, cols]), dot(a, wu_v[:, cols])
             v = 0.5 * jnp.tanh(0.5 * r) + 0.5
             silu = r * v
-            t_ring[slot, :, cols] = silu
-            q_ring[slot, :, cols] = s * (v + silu * (1.0 - v))
+            slope = s * (v + silu * (1.0 - v))
             act[m, rows, cols] = (silu * s).astype(bf16)
+            if by_ref is None:
+                t_ring[slot, :, cols] = silu
+                q_ring[slot, :, cols] = slope
+            else:
+                by = by_ref[:, cols].astype(f32)
+                b = lax.rem(i // per, 2)
+                du[b, rows, cols] = (silu * by).astype(bf16)
+                dg[b, rows, cols] = (slope * by).astype(bf16)
 
     def down(i):
         m, rows = lax.rem(i // per, held), chunk(lax.rem(i, per))
         y = dot(act[m, rows, :], wd_v[...]).astype(bf16)
         fwd_out[lax.rem(i, SENDS)] = (fwd_in[i].astype(f32) + y.astype(f32)).astype(bf16)
 
-    def forward_send(i):
-        @pl.when(~last)
-        def _():
-            onward(i).start()
-
-    def backward_wait(i):
-        @pl.when(last)
-        def _():
-            load_dy(i).wait()
-
-        @pl.when(~last)
-        def _():
-            back(i).wait_recv()
-
-        @pl.when(~first & (i >= SENDS))
-        def _():
-            back(i - SENDS).wait_send()
+    def by_hidden(i):
+        load_dy(i).wait()
+        by_y = bwd_in[i]
+        dy_t[lax.rem(i // per, 2), :, chunk(lax.rem(i, per))] = by_y.T
+        by_act[...] = dot(by_y, wd_t[...]).astype(bf16)
 
     def by_gate_up(i):
         slot, m, rows = lax.rem(i, ring), lax.rem(i // per, 2), chunk(lax.rem(i, per))
@@ -177,11 +178,6 @@
         by_h = (by_a * scale + (along * (scale * scale * scale * (-1.0 / d))) * wide).astype(bf16)
         bwd_out[lax.rem(i, SENDS)] = (bwd_in[i].astype(f32) + by_h.astype(f32)).astype(bf16)
 
-    def backward_send(i):
-        @pl.when(~first)
-        def _():
-            back(i).start()
-
     def weights(i):
         number, rows = i // per, chunk(lax.rem(i, per))
         m, w = lax.rem(number, 2), lax.rem(number, held)
@@ -189,39 +185,81 @@
             term = dot(left[rows, :], right[...]).astype(bf16).astype(f32)
             acc[n, rows, :] = jnp.where(number == 0, 0.0, acc[n, rows, :]) + term
 
+    def half():
+        m, w, mid = (micro - 1) % 2, (micro - 1) % held, tokens // 2
+        for n, cols, left, right in tiles(a_t.at[w], dy_t.at[m], dg.at[m], du.at[m], act.at[w]):
+            term = dot(left[:, :mid], right[:mid, cols])
+            for q in range(d // ROWS):
+                t_ring[(chunks + n * (d // ROWS) + q) % ring, :, cols] = term[q * ROWS:(q + 1) * ROWS]
+        act_out[...] = act[w, mid:, :]
+        a_out[...] = a_t[w, :, mid:]
+
     def step(i, carry):
         j = i - lag
         k = j - per
-        forth, backwards, heavy = i < chunks, (j >= 0) & (j < chunks), (k >= 0) & (k < chunks - per)
-
-        @pl.when(forth)
+        forth, backwards = i < chunks, (j >= 0) & (j < chunks)
+
+        @pl.when(last & forth)
+        def _():
+            onward(i).wait_recv()
+
+            @pl.when(i >= SENDS)
+            def _():
+                back(i - SENDS).wait_send()
+            gate_up(i, by_act)
+            by_input(i)
+            back(i).start()
+
+        @pl.when(~last & forth)
         def _():
             forward_wait(i)
             gate_up(i)
-
-            @pl.when(~last)
+            down(i)
+            onward(i).start()
+
+        @pl.when(first & (i == 2))
+        def _():
+            turn(wd_v, wd_t)
+
+        @pl.when(~last & backwards)
+        def _():
+            back(j).wait_recv()
+
+            @pl.when(~first & (j >= SENDS))
             def _():
-                down(i)
-            forward_send(i)
-
-        @pl.when(first & (i == 2))
-        def _():
-            turn(wd_v, wd_t)
-
-        @pl.when(backwards)
-        def _():
-            backward_wait(j)
-            by_gate_up(j)
+                back(j - SENDS).wait_send()
+
+            @pl.when(first)
+            def _():
+                by_gate_up(j)
 
             @pl.when(~first)
             def _():
+                by_gate_up(j)
                 by_input(j)
-            backward_send(j)
-
-        @pl.when(heavy)
-        def _():
-            weights(k)
+                back(j).start()
+
+        hurry = first & (j >= chunks - per)
+        low = jnp.where(hurry, chunks - 2 * per + 2 * (j - chunks + per), jnp.maximum(k, 0))
+        high = jnp.minimum(jnp.where(hurry, low + 2, k + 1), chunks - per)
+
+        def share(n, c):
+            weights(n)
+            return c
+        lax.fori_loop(low, high, share, 0)
+
+        @pl.when(last & (i < chunks - 1))
+        def _():
+            by_hidden(i + 1)
+
+        @pl.when(j == jnp.where(first, chunks - 2, chunks - 1))
+        def _():
+            half()
         return carry
+
+    @pl.when(last)
+    def _():
+        by_hidden(0)
 
     lax.fori_loop(0, chunks + max(LAGS), step, 0)
 
@@ -235,22 +273,25 @@
             back(chunks - SENDS + n).wait_send()
 
 
-def finish(w, m, acc, act, a_t, dg, du, dy_t, out_g, out_u, out_d, stage, turned, sem):
-    d = acc.shape[1]
+def finish(m, chunks, acc, act, a_t, dg, du, dy_t, t_ring, out_g, out_u, out_d, stage, turned, sem):
+    d, mid = acc.shape[1], act.shape[0]
     copies = []
-    for n, (left, right, out) in enumerate(((dy_t.at[m], act.at[w], out_d), (a_t.at[w], dg.at[m], out_g), (a_t.at[w], du.at[m], out_u))):
-        for q in range(0, d, ROWS):
-            rows = slice(q, q + ROWS)
-            term = dot(left[rows, :], right[...]).astype(bf16).astype(f32)
-            total = (acc[(n + 2) % 3, rows, :] + term).astype(bf16)
-            if n == 0:
-                turned[:, rows] = total.T
-                copy = pltpu.make_async_copy(turned.at[:, rows], out.at[0, :, rows], sem.at[n, q // ROWS])
+    for p, (n, cols, left, right) in enumerate(tiles(a_t, dy_t.at[m, :, mid:], dg.at[m, mid:, :], du.at[m, mid:, :], act)):
+        second = dot(left[...], right[:, cols])
+        for q in range(d // ROWS):
+            rows = slice(q * ROWS, (q + 1) * ROWS)
+            term = t_ring[(chunks + n * (d // ROWS) + q) % t_ring.shape[0], :, cols] + second[rows]
+            total = (acc[n, rows, cols] + term.astype(bf16).astype(f32)).astype(bf16)
+            if n == 2:
+                turned[cols, rows] = total.T
             else:
-                stage[n - 1, rows, :] = total
-                copy = pltpu.make_async_copy(stage.at[n - 1, rows, :], out.at[0, rows, :], sem.at[n, q // ROWS])
-            copy.start()
-            copies.append(copy)
+                stage[n, rows, cols] = total
+        if n == 2:
+            copy = pltpu.make_async_copy(turned.at[cols, :], out_d.at[0, cols, :], sem.at[p])
+        else:
+            copy = pltpu.make_async_copy(stage.at[n, :, cols], (out_g, out_u)[n].at[0, :, cols], sem.at[p])
+        copy.start()
+        copies.append(copy)
     for copy in copies:
         copy.wait()
 
@@ -270,21 +311,24 @@
             functools.partial(kernel, stages, micro, tokens),
             out_shape=(
                 pltpu.VMEM((3, d, ff), f32),
-                pltpu.VMEM((held, tokens, ff), bf16),
-                pltpu.VMEM((held, d, tokens), bf16),
+                pltpu.VMEM((tokens // 2, ff), bf16),
+                pltpu.VMEM((d, tokens // 2), bf16),
                 pltpu.VMEM((2, tokens, ff), bf16),
                 pltpu.VMEM((2, tokens, ff), bf16),
                 pltpu.VMEM((2, d, tokens), bf16),
+                pltpu.VMEM((ring, ROWS, ff), f32),
             ),
             in_specs=[hbm] * 5,
-            out_specs=(vmem,) * 6,
+            out_specs=(vmem,) * 7,
             scratch_shapes=[
                 pltpu.VMEM((chunks, ROWS, d), bf16),
                 pltpu.VMEM((chunks, ROWS, d), bf16),
                 pltpu.VMEM((SENDS, ROWS, d), bf16),
                 pltpu.VMEM((SENDS, ROWS, d), bf16),
                 pltpu.VMEM((ring, ROWS, ff), f32),
-                pltpu.VMEM((ring, ROWS, ff), f32),
+                pltpu.VMEM((ROWS, ff), bf16),
+                pltpu.VMEM((held, tokens, ff), bf16),
+                pltpu.VMEM((held, d, tokens), bf16),
                 pltpu.VMEM((d, ff), bf16),
                 pltpu.VMEM((d, ff), bf16),
                 pltpu.VMEM((ff, d), bf16),
@@ -297,18 +341,18 @@
                 pltpu.SemaphoreType.DMA((SENDS,)),
                 pltpu.SemaphoreType.DMA((3,)),
             ],
-            compiler_params=pltpu.CompilerParams(collective_id=0, has_side_effects=True, vmem_limit_bytes=38 * 2**20),
+            compiler_params=pltpu.CompilerParams(collective_id=0, has_side_effects=True, vmem_limit_bytes=39 * 2**20),
         )(x, dy, wg, wu, wd)
         return pl.pallas_call(
-            functools.partial(finish, (micro - 1) % held, (micro - 1) % 2),
+            functools.partial(finish, (micro - 1) % 2, chunks),
             out_shape=(
                 jax.ShapeDtypeStruct((1, d, ff), bf16),
                 jax.ShapeDtypeStruct((1, d, ff), bf16),
                 jax.ShapeDtypeStruct((1, ff, d), bf16),
             ),
-            in_specs=[vmem] * 6,
+            in_specs=[vmem] * 7,
             out_specs=(hbm,) * 3,
-            scratch_shapes=[pltpu.VMEM((2, d, ff), bf16), pltpu.VMEM((ff, d), bf16), pltpu.SemaphoreType.DMA((3, d // ROWS))],
+            scratch_shapes=[pltpu.VMEM((2, d, ff), bf16), pltpu.VMEM((ff, d), bf16), pltpu.SemaphoreType.DMA((3 * (ff // COLS),))],
             compiler_params=pltpu.CompilerParams(has_side_effects=True, vmem_limit_bytes=8 * 2**20),
         )(*sums)
 

time: 131 us -> 129 us (0.985)
  Pallas kernels: 130 us -> 128 us
    pallas_call x1, Pallas kernels: 127 us -> 125 us  [step(): pl.pallas_call(functools.partial(kernel, stages, micro, tokens), out_shap...]
where the time goes in v2:
time: 129 us; the launch traced here: 128 us
  Pallas kernels  128 us (99%)
    pallas_call x1, Pallas kernels, step(): pl.pallas_call(functools.partial(kernel, stages, micro, tokens), out_shap...  125 us
    pallas_call x1, Pallas kernels, step(): pl.pallas_call(functools.partial(finish, (micro - 1) % 2, chunks), out_sh...  2.73 us

profile of v2, /device:TPU:120, one launch (start us, length us, event | category | flops | bytes accessed | tf_op | source)
XLA Modules:
  0.0 128.5 jit_solution(13834509036112496368)
XLA Ops:
  0.6 125.1 %shard_map.76 = (f32[3,512,1280]{2,1,0:T(8,128)S(1)}, bf16[256,1280]{1,0:T(8,128)(2,1)S(1)}, bf16[512,256]{1,0:T(8,128)(2,1)S(1)}, bf16[2,512,1280]{2,1,0:T(8,12...) custom-call(bf16[8,512,512]{2,1,0:T(8,128)(2,1)} %x.1, ...), custom_call_target="tpu_custom_call" | custom-call | tf_op jit(solution)/shard_map/pallas_call | solution.py:310
  125.7 2.7 %shard_map.77 = (bf16[1,512,1280]{2,1,0:T(8,128)(2,1)}, bf16[1,512,1280]{2,1,0:T(8,128)(2,1)}, bf16[1,1280,512]{2,1,0:T(8,128)(2,1)}) custom-call(f32[3,512,1280]{2,1,0:T(8,128)S(1)} %get-tuple-element.10.acc, bf16[256,1280]{1,0:T(8,128)(2,1)S(1)} %get-tuple-element.11.act, bf16[512,256]{1,0:T(8,128)(2,1)S(1)} %get-tuple-element.12.a_t, ...), custom_call_target="tpu_custom_call" | custom-call | tf_op jit(solution)/shard_map/pallas_call | solution.py:346

commit v3 on v2

--- a/solution.py
+++ b/solution.py
@@ -11,6 +11,7 @@
 ROWS = 128
 COLS = 256
 LAGS = (13,8,4,0)
+STAGGER = 800
 SENDS = 3
 f32, bf16 = jnp.float32, jnp.bfloat16
 
@@ -239,9 +240,10 @@
                 by_input(j)
                 back(j).start()
 
-        hurry = first & (j >= chunks - per)
-        low = jnp.where(hurry, chunks - 2 * per + 2 * (j - chunks + per), jnp.maximum(k, 0))
-        high = jnp.minimum(jnp.where(hurry, low + 2, k + 1), chunks - per)
+        ending = j >= chunks - per
+        done = chunks - per
+        low = jnp.where(ending, jnp.where(first, 2 * j - chunks, done - per), jnp.maximum(k, 0))
+        high = jnp.where(ending, jnp.where(first, jnp.minimum(2 * j - chunks + 2, done), jnp.where(j == chunks - 1, done, 0)), k + 1)
 
         def share(n, c):
             weights(n)
@@ -261,6 +263,10 @@
     def _():
         by_hidden(0)
 
+    @pl.when(first & (lax.rem(lax.axis_index("rep"), 2) == 0))
+    def _():
+        pl.delay(STAGGER)
+
     lax.fori_loop(0, chunks + max(LAGS), step, 0)
 
     for n in range(SENDS):
@@ -277,10 +283,9 @@
     d, mid = acc.shape[1], act.shape[0]
     copies = []
     for p, (n, cols, left, right) in enumerate(tiles(a_t, dy_t.at[m, :, mid:], dg.at[m, mid:, :], du.at[m, mid:, :], act)):
-        second = dot(left[...], right[:, cols])
         for q in range(d // ROWS):
             rows = slice(q * ROWS, (q + 1) * ROWS)
-            term = t_ring[(chunks + n * (d // ROWS) + q) % t_ring.shape[0], :, cols] + second[rows]
+            term = t_ring[(chunks + n * (d // ROWS) + q) % t_ring.shape[0], :, cols] + dot(left[rows, :], right[:, cols])
             total = (acc[n, rows, cols] + term.astype(bf16).astype(f32)).astype(bf16)
             if n == 2:
                 turned[cols, rows] = total.T

time: 129 us -> 128 us (level)
  no operation moved by 1% of the time
where the time goes in v3:
time: 128 us
  Pallas kernels  127 us (99%)
    pallas_call x1, Pallas kernels, step(): pl.pallas_call(functools.partial(kernel, stages, micro, tokens), out_shap...  125 us
    pallas_call x1, Pallas kernels, step(): pl.pallas_call(functools.partial(finish, (micro - 1) % 2, chunks), out_sh...  2.67 us

profile of v3, /device:TPU:120, one launch (start us, length us, event | category | flops | bytes accessed | tf_op | source)
XLA Modules:
  0.0 127.8 jit_solution(3835784858179504657)
XLA Ops:
  0.6 124.5 %shard_map.76 = (f32[3,512,1280]{2,1,0:T(8,128)S(1)}, bf16[256,1280]{1,0:T(8,128)(2,1)S(1)}, bf16[512,256]{1,0:T(8,128)(2,1)S(1)}, bf16[2,512,1280]{2,1,0:T(8,12...) custom-call(bf16[8,512,512]{2,1,0:T(8,128)(2,1)} %x.1, ...), custom_call_target="tpu_custom_call" | custom-call | tf_op jit(solution)/shard_map/pallas_call | solution.py:315
  125.2 2.7 %shard_map.77 = (bf16[1,512,1280]{2,1,0:T(8,128)(2,1)}, bf16[1,512,1280]{2,1,0:T(8,128)(2,1)}, bf16[1,1280,512]{2,1,0:T(8,128)(2,1)}) custom-call(f32[3,512,1280]{2,1,0:T(8,128)S(1)} %get-tuple-element.10.acc, bf16[256,1280]{1,0:T(8,128)(2,1)S(1)} %get-tuple-element.11.act, bf16[512,256]{1,0:T(8,128)(2,1)S(1)} %get-tuple-element.12.a_t, ...), custom_call_target="tpu_custom_call" | custom-call | tf_op jit(solution)/shard_map/pallas_call | solution.py:351

commit v4 on v3

--- a/solution.py
+++ b/solution.py
@@ -11,7 +11,8 @@
 ROWS = 128
 COLS = 256
 LAGS = (13,8,4,0)
-STAGGER = 800
+LATE_LAGS = (13, 7, 3, 0)
+STAGGER = 4000
 SENDS = 3
 f32, bf16 = jnp.float32, jnp.bfloat16
 
@@ -41,7 +42,8 @@
     d, ff = wg_v.shape
     ring, held = t_ring.shape[0], act.shape[0]
     first, last = me == 0, me == stages - 1
-    lag = sum(jnp.where(me == n, by, 0) for n, by in enumerate(LAGS))
+    late = lax.rem(lax.axis_index("rep"), 2) == 1
+    lag = sum(jnp.where(me == n, jnp.where(late, a, b), 0) for n, (a, b) in enumerate(zip(LATE_LAGS, LAGS)))
 
     def load_x(i):
         return pltpu.make_async_copy(x.at[i // per, chunk(lax.rem(i, per)), :], fwd_in.at[i], fwd_sem.at[i])
@@ -263,7 +265,7 @@
     def _():
         by_hidden(0)
 
-    @pl.when(first & (lax.rem(lax.axis_index("rep"), 2) == 0))
+    @pl.when(first & late)
     def _():
         pl.delay(STAGGER)
 

time: 128 us -> 131 us (1.023)
  the two profiles are of different devices: /device:TPU:120 before, /device:TPU:121 now
where the time goes in v4:
time: 131 us
  Pallas kernels  130 us (99%)
    pallas_call x1, Pallas kernels, step(): pl.pallas_call(functools.partial(kernel, stages, micro, tokens), out_shap...  127 us
    pallas_call x1, Pallas kernels, step(): pl.pallas_call(functools.partial(finish, (micro - 1) % 2, chunks), out_sh...  2.68 us

profile of v4, /device:TPU:121, one launch (start us, length us, event | category | flops | bytes accessed | tf_op | source)
XLA Modules:
  0.0 130.8 jit_solution(11398305119798938622)
XLA Ops:
  0.6 127.4 %shard_map.76 = (f32[3,512,1280]{2,1,0:T(8,128)S(1)}, bf16[256,1280]{1,0:T(8,128)(2,1)S(1)}, bf16[512,256]{1,0:T(8,128)(2,1)S(1)}, bf16[2,512,1280]{2,1,0:T(8,12...) custom-call(bf16[8,512,512]{2,1,0:T(8,128)(2,1)} %x.1, ...), custom_call_target="tpu_custom_call" | custom-call | tf_op jit(solution)/shard_map/pallas_call | solution.py:317
  128.1 2.7 %shard_map.77 = (bf16[1,512,1280]{2,1,0:T(8,128)(2,1)}, bf16[1,512,1280]{2,1,0:T(8,128)(2,1)}, bf16[1,1280,512]{2,1,0:T(8,128)(2,1)}) custom-call(f32[3,512,1280]{2,1,0:T(8,128)S(1)} %get-tuple-element.10.acc, bf16[256,1280]{1,0:T(8,128)(2,1)S(1)} %get-tuple-element.11.act, bf16[512,256]{1,0:T(8,128)(2,1)S(1)} %get-tuple-element.12.a_t, ...), custom_call_target="tpu_custom_call" | custom-call | tf_op jit(solution)/shard_map/pallas_call | solution.py:353
